TPU v7x, 256 devices: a whole 4x4x8 slice. The times are simulated.
256 devices in a mesh: row: 8 (over z), col: 8 (over y, core), depth: 4 (over x).
Axes of the slice: x: 4, y: 4, z: 8, core: 2. Of those that a mesh axis runs over, the one named last changes fastest.
Arguments:
- a21_leaf: float32 [4, 4096, 2048], P('depth', 'row', 'col'), may hold values from -1.2 to 1.2
- a12_leaf: float32 [4, 2048, 4096], P('depth', 'row', 'col'), may hold values from -1.2 to 1.2
- uinv_leaf: float32 [4, 2048, 2048], P('depth', None, 'col'), may hold values from -0.2 to 1.5, as said below
- linv_leaf: float32 [4, 2048, 2048], P('depth', 'row'), may hold values from -0.2 to 1.5, as said below
- live: int32 [4], P('depth'), may hold values from 16 to 32
- row_map: int32 [4, 32], P('depth', 'row'), may hold values from 0 to 63, as said below
- col_map: int32 [4, 32], P('depth', 'col'), may hold values from 0 to 63, as said below
- a22_anc: float32 [8192, 8192], P(('row', 'depth'), 'col'), may hold values from -6 to 6
- a21_anc: float32 [8192, 2048], P(('row', 'depth'), 'col'), may hold values from -1.2 to 1.2
- a12_anc: float32 [2048, 8192], P(('row', 'depth'), 'col'), may hold values from -1.2 to 1.2
- uinv_anc: float32 [2048, 2048], P(None, 'col'), may hold values from -0.2 to 1.5, as said below
- linv_anc: float32 [2048, 2048], P(('row', 'depth')), may hold values from -0.2 to 1.5, as said below
Outputs:
- leaf_lower: float32 [4, 4096, 2048], P('depth', 'row', 'col')
- leaf_upper: float32 [4, 2048, 4096], P('depth', 'row', 'col')
- anc_lower: float32 [8192, 2048], P(('row', 'depth'), 'col')
- anc_upper: float32 [2048, 8192], P(('row', 'depth'), 'col')
- anc_schur: float32 [8192, 8192], P(('row', 'depth'), 'col')
Inputs may be any that keep to these rules, and one draw needn't show every extreme that they name: `uinv_leaf`: upper triangular: zero below the diagonal, diagonal between 0.5 and 1.5. `linv_leaf`: lower triangular: zero above the diagonal, diagonal between 0.5 and 1.5. `uinv_anc`: upper triangular: zero below the diagonal, diagonal between 0.5 and 1.5. `linv_anc`: lower triangular: zero above the diagonal, diagonal between 0.5 and 1.5. `row_map`: within one replica the entries are distinct. Leaf block row i lies in the k-th of 8 equal ranges of leaf block rows, and its target lies in the k-th of 8 equal ranges of the 64 ancestor block rows. `col_map`: within one replica the entries are distinct. Leaf block column j lies in the k-th of 8 equal ranges of leaf block columns, and its target lies in the k-th of 8 equal ranges of the 64 ancestor block columns.
All inputs are finite; a program needn't handle non-finite values.
Results may differ from a plain program's by a relative error of at most 0.0001.
Values sent between devices are 32-bit elements; how exact they have to be, the bound alone decides.
No kernel may reach another device: no remote copies, remote signals or barrier semaphores. Data moves between devices by JAX's collectives and lax.ppermute only.
A program may use at most 128 MiB of HBM per device.

v0:
```python
import math
import jax
import jax.numpy as jnp
from jax import lax
from jax.sharding import PartitionSpec as P

NB = 128


def in_one_piece(arrays, axis, split_dim, concat_dim, along):
    widths = [math.prod(a.shape[along:]) for a in arrays]
    both = jnp.concatenate(
        [a.reshape(*a.shape[:along], w) for a, w in zip(arrays, widths)], axis=along
    )
    out = lax.all_to_all(both, axis, split_axis=split_dim, concat_axis=concat_dim, tiled=True)
    tiles = jnp.split(out, [sum(widths[:k]) for k in range(1, len(widths))], axis=along)
    return tuple((b.reshape(*out.shape[:along], *a.shape[along:]) for a, b in zip(arrays, tiles)))


def sent_to_all(shard, axis):
    copies = jnp.broadcast_to(shard, (lax.axis_size(axis), *shard.shape))
    return lax.all_to_all(copies, axis, split_axis=0, concat_axis=0, tiled=True)


def in_order(tiles, dim):
    lengths = list(tiles.shape[1:])
    lengths[dim] *= tiles.shape[0]
    return jnp.moveaxis(tiles, 0, dim).reshape(lengths)


def collect(shard, axis, dim):
    tiles = sent_to_all(shard, axis)
    return in_order(tiles, dim)


def gather_axes(shard, axes, dim):
    out = shard
    for number in range(len(axes) - 1, -1, -1):
        out = lax.all_gather(out, axes[number], axis=dim, tiled=True)
    return out


def product(left, right):
    return jnp.dot(left, right, precision=lax.Precision.HIGHEST, preferred_element_type=jnp.float32)


def combine_depth(schur, row_map, col_map, a22_anc):
    block_size = NB
    rows_here = schur.shape[0]
    cols_here = schur.shape[1]
    leaf_rows = rows_here // block_size
    leaf_cols = cols_here // block_size
    anc_rows = a22_anc.shape[0]
    replicas = lax.axis_size("depth")
    anc_row_blocks = anc_rows * replicas // block_size
    anc_col_blocks = a22_anc.shape[1] // block_size
    row_local = row_map[0] - lax.axis_index("row") * anc_row_blocks
    col_local = col_map[0] - lax.axis_index("col") * anc_col_blocks
    owner_blocks = anc_rows // block_size
    slots = min(leaf_rows, owner_blocks)
    owner = row_local // owner_blocks
    earlier = lax.iota(jnp.int32, leaf_rows)[:, None] > lax.iota(jnp.int32, leaf_rows)[None, :]
    same = owner[:, None] == owner[None, :]
    rank = jnp.sum((earlier & same).astype(jnp.int32), axis=1)
    select = (
        (owner[:, None, None] == lax.iota(jnp.int32, replicas)[None, :, None])
        & (rank[:, None, None] == lax.iota(jnp.int32, slots)[None, None, :])
    ).astype(jnp.float32)
    leaf_blocks = schur.reshape(leaf_rows, block_size, cols_here)
    packed = jnp.einsum("iqs,ixc->qsxc", select, leaf_blocks, precision=lax.Precision.HIGHEST)
    packed = packed.reshape(replicas, slots * block_size, cols_here)
    target = (row_local - owner * owner_blocks + 1).astype(jnp.float32)
    tags = jnp.einsum("iqs,i->qs", select, target, precision=lax.Precision.HIGHEST) - 1.0
    col_tags = jnp.broadcast_to(col_local.astype(jnp.float32)[None, :], (replicas, leaf_cols))
    got_rows, got_tags, got_cols = in_one_piece((packed, tags, col_tags), "depth", 0, 0, 1)
    slot_pick = (
        got_tags[:, :, None] == lax.iota(jnp.int32, owner_blocks).astype(jnp.float32)[None, None, :]
    ).astype(jnp.float32)
    column_pick = (
        got_cols[:, :, None]
        == lax.iota(jnp.int32, anc_col_blocks).astype(jnp.float32)[None, None, :]
    ).astype(jnp.float32)
    pieces = got_rows.reshape(replicas, slots, block_size, leaf_cols, block_size)
    sectioned = jnp.einsum("psa,psxjy->paxjy", slot_pick, pieces, precision=lax.Precision.HIGHEST)
    placed = jnp.einsum("paxjy,pjb->axby", sectioned, column_pick, precision=lax.Precision.HIGHEST)
    return placed.reshape(anc_rows, anc_col_blocks * block_size)


def anc_panels(a21_anc, a12_anc, uinv_anc, linv_anc):
    factor = uinv_anc
    anc_lower = product(collect(a21_anc, "col", 1), factor)
    lower_whole = collect(anc_lower, "col", 1)
    factor = linv_anc
    anc_upper = product(factor, lax.all_gather(a12_anc, ("row", "depth"), axis=0, tiled=True))
    return (anc_lower, lower_whole, anc_upper)


def shards(
    a21_leaf,
    a12_leaf,
    uinv_leaf,
    linv_leaf,
    live,
    row_map,
    col_map,
    a22_anc,
    a21_anc,
    a12_anc,
    uinv_anc,
    linv_anc,
):
    block_size = NB
    panel_left = a21_leaf[0]
    panel_top = a12_leaf[0]
    upper_inverse = uinv_leaf[0]
    lower_inverse = linv_leaf[0]
    rows_here = panel_left.shape[0]
    cols_here = panel_top.shape[1]
    live_rows = live[0] * block_size
    row_pos = lax.axis_index("row") * rows_here + lax.iota(jnp.int32, rows_here)
    col_pos = lax.axis_index("col") * cols_here + lax.iota(jnp.int32, cols_here)
    row_keep = (row_pos < live_rows).astype(jnp.float32)
    col_keep = (col_pos < live_rows).astype(jnp.float32)
    factor = upper_inverse
    lower_part = product(lax.all_gather(panel_left, "col", axis=1, tiled=True), factor)
    leaf_lower = lower_part * row_keep[:, None]
    factor = lower_inverse
    upper_part = product(factor, lax.all_gather(panel_top, "row", axis=0, tiled=True))
    leaf_upper = upper_part * col_keep[None, :]
    upper_whole = lax.all_gather(leaf_upper, "row", axis=0, tiled=True)
    factor = upper_whole
    schur = jnp.zeros((rows_here, cols_here), jnp.float32) - product(
        lax.all_gather(leaf_lower, "col", axis=1, tiled=True), factor
    )
    own_update = combine_depth(schur, row_map, col_map, a22_anc)
    anc_lower, lower_whole, anc_upper = anc_panels(a21_anc, a12_anc, uinv_anc, linv_anc)
    factor = lower_whole
    anc_schur = a22_anc + own_update - product(factor, gather_axes(anc_upper, ("row", "depth"), 0))
    return (leaf_lower[None], leaf_upper[None], anc_lower, anc_upper, anc_schur)


def solution(mesh):
    in_specs = (
        P("depth", "row", "col"),
        P("depth", "row", "col"),
        P("depth", None, "col"),
        P("depth", "row", None),
        P("depth"),
        P("depth", "row"),
        P("depth", "col"),
        P(("row", "depth"), "col"),
        P(("row", "depth"), "col"),
        P(("row", "depth"), "col"),
        P(None, "col"),
        P(("row", "depth"), None),
    )
    out_specs = (
        P("depth", "row", "col"),
        P("depth", "row", "col"),
        P(("row", "depth"), "col"),
        P(("row", "depth"), "col"),
        P(("row", "depth"), "col"),
    )
    return jax.shard_map(shards, mesh=mesh, in_specs=in_specs, out_specs=out_specs, check_vma=False)
```

profile of v0, /device:TPU:1, one launch (start us, length us, event | category | flops | bytes accessed | tf_op | source)
XLA Modules:
  0.0 436.7 jit_solution(4254180319421357973)
XLA Ops:
  10.1 38.6 %all-gather.20.cloned.1.call-done = f32[1,512,2048]{2,1,0:T(8,128)} async-done(((f32[1,512,256]{2,1,0:T(8,128)}), f32[1,512,2048]{2,1,0:T(8,128)}) %all-gather.20.cloned.1.call-update) | async-done | bytes 4194320 | tf_op jit(solution)/shard_map/all_gather | solution.py:125
  48.7 6.4 %fusion.10 = f32[512,256]{1,0:T(8,128)} fusion(f32[1,2048,256]{2,1,0:T(8,128)S(1)} %copy-done, f32[1,512,2048]{2,1,0:T(8,128)} %all-gather.20.cloned.1.call-done, f32[512]{0:T(512)S(1)} %fusion.32), kind=kOutput, calls=%fused_computation.13 | convolution fusion | flops 3221356544 | bytes 6817792 | tf_op jit(solution)/shard_map/dot_general | solution.py:44
  55.2 49.4 %all-gather.22.cloned.1.call-done = f32[1,2048,512]{2,1,0:T(8,128)} async-done(((f32[1,256,512]{2,1,0:T(8,128)}), f32[1,2048,512]{2,1,0:T(8,128)}) %all-gather.22.cloned.1.call-update) | async-done | bytes 4194320 | tf_op jit(solution)/shard_map/all_gather | solution.py:128
  104.6 7.3 %fusion.15 = f32[256,512]{1,0:T(8,128)} fusion(f32[1,2048,512]{2,1,0:T(8,128)} %all-gather.22.cloned.1.call-done, f32[1,256,2048]{2,1,0:T(8,128)} %param.15, f32[512]{0:T(512)S(1)} %fusion.33), kind=kOutput, calls=%fused_computation.14 | convolution fusion | flops 3221356544 | bytes 6817792 | tf_op jit(solution)/shard_map/dot_general | solution.py:44
  113.6 5.3 %all-to-all-start = ((f32[8,256,256]{1,2,0:T(8,128)}), f32[8,256,256]{1,2,0:T(8,128)S(1)}, u32[]{:S(2)}, u32[]{:S(2)}) async-start(f32[8,256,256]{1,2,0:T(8,128)} %broadcast_in_dim.16), calls=%async_computation | async-start | bytes 4194304 | tf_op jit(solution)/shard_map/all_to_all | solution.py:22
  119.0 84.1 %all-gather.10.cloned.1.call-done = f32[2048,1024]{1,0:T(8,128)} async-done(((f32[64,1024]{1,0:T(8,128)}), f32[2048,1024]{1,0:T(8,128)}) %all-gather.10.cloned.1.call-update) | async-done | bytes 8388624 | tf_op jit(solution)/shard_map/all_gather | solution.py:94
  203.1 8.2 %fusion.51 = f32[64,1024]{1,0:T(8,128)} fusion(f32[64,2048]{1,0:T(8,128)S(1)} %copy-done.3, f32[2048,1024]{1,0:T(8,128)} %all-gather.10.cloned.1.call-done), kind=kOutput, calls=%fused_computation.69 | convolution fusion | flops 1610612736 | bytes 9175040 | tf_op jit(solution)/shard_map/dot_general | solution.py:44
  211.9 26.4 %all-gather.12.cloned.1.call-done = f32[512,2048]{1,0:T(8,128)} async-done(((f32[512,256]{1,0:T(8,128)}), f32[512,2048]{1,0:T(8,128)}) %all-gather.12.cloned.1.call-update) | async-done | bytes 4194320 | tf_op jit(solution)/shard_map/all_gather | solution.py:133
  238.3 56.4 %all-gather.14.cloned.1.call-done = f32[2048,512]{1,0:T(8,128)} async-done(((f32[256,512]{1,0:T(8,128)}), f32[2048,512]{1,0:T(8,128)}) %all-gather.14.cloned.1.call-update) | async-done | bytes 4194320 | tf_op jit(solution)/shard_map/all_gather | solution.py:130
  294.7 9.4 %convolution_subtract_fusion = f32[512,512]{1,0:T(8,128)S(1)} fusion(f32[512,2048]{1,0:T(8,128)} %all-gather.12.cloned.1.call-done, f32[2048,512]{1,0:T(8,128)} %all-gather.14.cloned.1.call-done), kind=kOutput, calls=%fused_computation.11 | convolution fusion | flops 6442713088 | bytes 9437184 | tf_op jit(solution)/shard_map/dot_general | solution.py:44
  304.0 3.6 fusion.20
  307.6 12.7 %all-gather.16.cloned.1.call-done = f32[256,1024]{1,0:T(8,128)} async-done(((f32[64,1024]{1,0:T(8,128)}), f32[256,1024]{1,0:T(8,128)}) %all-gather.16.cloned.1.call-update) | async-done | bytes 1048592 | tf_op jit(solution)/shard_map/all_gather | solution.py:39
  320.3 3.1 constant_dynamic-update-slice_fusion
  326.0 4.8 %copy.31 = f32[4,1,131078]{2,1,0:T(1,128)} copy(f32[4,1,131078]{2,0,1:T(4,128)} %bitcast.99) | data formatting | bytes 4194496 | tf_op jit(solution)/shard_map/all_to_all | solution.py:15
  330.9 4.5 %all-to-all-start.1 = ((f32[4,1,131078]{2,1,0:T(1,128)}), f32[4,1,131078]{2,1,0:T(1,128)}, u32[]{:S(2)}, u32[]{:S(2)}) async-start(f32[4,1,131078]{2,1,0:T(1,128)} %copy.31), calls=%async_computation.1 | async-start | bytes 4198400 | tf_op jit(solution)/shard_map/all_to_all | solution.py:15
  335.4 5.3 %fusion.50 = f32[256,256]{1,0:T(8,128)S(1)} fusion(f32[256,2048]{0,1:T(8,128)S(1)} %bitcast.100, f32[2048,256]{1,0:T(8,128)} %param.22), kind=kOutput, calls=%fused_computation.68 | convolution fusion | flops 1610612736 | bytes 4456448 | tf_op jit(solution)/shard_map/dot_general | solution.py:44
  340.8 18.3 %all-to-all-done.1 = f32[4,1,131078]{2,1,0:T(1,128)} async-done(((f32[4,1,131078]{2,1,0:T(1,128)}), f32[4,1,131078]{2,1,0:T(1,128)}, u32[]{:S(2)}, u32[]{:S(2)}) %all-to-all-start.1) | async-done | bytes 2097280 | tf_op jit(solution)/shard_map/all_to_all | solution.py:15
  360.6 7.9 %all-to-all-start.2 = ((f32[8,256,256]{1,2,0:T(8,128)}), f32[8,256,256]{1,2,0:T(8,128)}, u32[]{:S(2)}, u32[]{:S(2)}) async-start(f32[8,256,256]{1,2,0:T(8,128)} %broadcast_in_dim.20), calls=%async_computation.2 | async-start | bytes 4194304 | tf_op jit(solution)/shard_map/all_to_all | solution.py:22
  372.8 3.4 reshape_reshape.7
  376.2 4.8 %fusion.8 = f32[4,2,128,4,128]{4,1,3,2,0:T(2,128)S(1)} fusion(f32[4,2,128,4,128]{4,3,2,1,0:T(4,128)S(1)} %reshape_reshape.7, f32[4,2]{1,0:T(4,128)S(1)} %split.13, f32[2]{0:T(128)S(1)} %iota_convert_fusion), kind=kOutput, calls=%fused_computation.9 | convolution fusion | flops 12582928 | bytes 4194344 | tf_op jit(solution)/shard_map/psa,psxjy->paxjy/dot_general | solution.py:84
  381.0 3.2 fusion.6
  384.3 10.6 %all-to-all-done.2 = f32[8,256,256]{1,2,0:T(8,128)} async-done(((f32[8,256,256]{1,2,0:T(8,128)}), f32[8,256,256]{1,2,0:T(8,128)}, u32[]{:S(2)}, u32[]{:S(2)}) %all-to-all-start.2) | async-done | bytes 2097184 | tf_op jit(solution)/shard_map/all_to_all | solution.py:22
  394.8 23.6 %all-gather.18.cloned.1.call-done = f32[2048,1024]{1,0:T(8,128)} async-done(((f32[256,1024]{1,0:T(8,128)}), f32[2048,1024]{1,0:T(8,128)}) %all-gather.18.cloned.1.call-update) | async-done | bytes 8388624 | tf_op jit(solution)/shard_map/all_gather | solution.py:39
  418.5 11.4 %convolution_subtract_fusion.1 = f32[256,1024]{1,0:T(8,128)} fusion(f32[256,2048]{0,1:T(8,128)} %bitcast.28, f32[2048,1024]{1,0:T(8,128)} %all-gather.18.cloned.1.call-done, f32[256,1024]{1,0:T(8,128)} %param.19, f32[32,8,8,128]{3,2,1,0:T(8,128)S(1)} %bitcast.103), kind=kOutput, calls=%fused_computation.12 | convolution fusion | flops 6442975232 | bytes 13631488 | tf_op jit(solution)/shard_map/dot_general | solution.py:44
  (54 shorter events, 13.2 us)
Async XLA Ops:
  7.2 41.5 %copy-start = (f32[1,2048,256]{2,1,0:T(8,128)S(1)}, f32[1,2048,256]{2,1,0:T(8,128)}, u32[]{:S(2)}) copy-start(f32[1,2048,256]{2,1,0:T(8,128)} %param.14) | copy-start | bytes 6291460
  7.2 41.5 %all-gather.20.cloned.1.call-start = ((), (), s32[]{:S(2)}) async-start(), calls=%async_computation.8 | async-start | bytes 4718592 | tf_op jit(solution)/shard_map/all_gather | solution.py:125
  7.9 96.7 %all-gather.22.cloned.1.call-start = ((), (), s32[]{:S(2)}) async-start(), calls=%async_computation.9 | async-start | bytes 4718592 | tf_op jit(solution)/shard_map/all_gather | solution.py:128
  8.7 194.5 %all-gather.10.cloned.1.call-start = ((), (), s32[]{:S(2)}) async-start(), calls=%async_computation.3 | async-start | bytes 8650752 | tf_op jit(solution)/shard_map/all_gather | solution.py:94
  9.4 228.9 %all-gather.12.cloned.1.call-start = ((), (), s32[]{:S(2)}) async-start(), calls=%async_computation.4 | async-start | bytes 4718592 | tf_op jit(solution)/shard_map/all_gather | solution.py:133
  55.1 239.5 %all-gather.14.cloned.1.call-start = ((), (), s32[]{:S(2)}) async-start(), calls=%async_computation.5 | async-start | bytes 4718592 | tf_op jit(solution)/shard_map/all_gather | solution.py:130
  55.2 56.8 %copy-start.4 = (f32[256,256]{1,0:T(8,128)S(1)}, f32[256,256]{1,0:T(8,128)}, u32[]{:S(2)}) copy-start(f32[256,256]{1,0:T(8,128)} %param.20) | copy-start | bytes 786436
  113.6 5.3 %copy-start.5 = (s32[1,4]{1,0:T(1,128)S(1)}, s32[1,4]{1,0:T(1,128)}, u32[]{:S(2)}) copy-start(s32[1,4]{1,0:T(1,128)} %param.17) | copy-start | bytes 52
  113.6 89.5 %copy-start.3 = (f32[64,2048]{1,0:T(8,128)S(1)}, f32[64,2048]{1,0:T(8,128)}, u32[]{:S(2)}) copy-start(f32[64,2048]{1,0:T(8,128)} %param.23) | copy-start | bytes 1572868
  113.6 217.2 %all-to-all-start = ((f32[8,256,256]{1,2,0:T(8,128)}), f32[8,256,256]{1,2,0:T(8,128)S(1)}, u32[]{:S(2)}, u32[]{:S(2)}) async-start(f32[8,256,256]{1,2,0:T(8,128)} %broadcast_in_dim.16), calls=%async_computation | async-start | bytes 4194304 | tf_op jit(solution)/shard_map/all_to_all | solution.py:22
  118.9 201.4 %all-gather.16.cloned.1.call-start = ((), (), s32[]{:S(2)}) async-start(), calls=%async_computation.6 | async-start | bytes 1310720 | tf_op jit(solution)/shard_map/all_gather | solution.py:39
  119.0 92.8 %copy-start.6 = (s32[1,4]{1,0:T(1,128)S(1)}, s32[1,4]{1,0:T(1,128)}, u32[]{:S(2)}) copy-start(s32[1,4]{1,0:T(1,128)} %param.18) | copy-start | bytes 52
  211.4 207.1 %all-gather.18.cloned.1.call-start = ((), (), s32[]{:S(2)}) async-start(), calls=%async_computation.7 | async-start | bytes 9437184 | tf_op jit(solution)/shard_map/all_gather | solution.py:39
  330.9 28.3 %all-to-all-start.1 = ((f32[4,1,131078]{2,1,0:T(1,128)}), f32[4,1,131078]{2,1,0:T(1,128)}, u32[]{:S(2)}, u32[]{:S(2)}) async-start(f32[4,1,131078]{2,1,0:T(1,128)} %copy.31), calls=%async_computation.1 | async-start | bytes 4198400 | tf_op jit(solution)/shard_map/all_to_all | solution.py:15
  340.7 20.0 %copy-start.2 = (f32[256,256]{1,0:T(8,128)}, f32[256,256]{1,0:T(8,128)S(1)}, u32[]{:S(2)}) copy-start(f32[256,256]{1,0:T(8,128)S(1)} %fusion.50) | copy-start | bytes 786436
  360.6 34.2 %all-to-all-start.2 = ((f32[8,256,256]{1,2,0:T(8,128)}), f32[8,256,256]{1,2,0:T(8,128)}, u32[]{:S(2)}, u32[]{:S(2)}) async-start(f32[8,256,256]{1,2,0:T(8,128)} %broadcast_in_dim.20), calls=%async_computation.2 | async-start | bytes 4194304 | tf_op jit(solution)/shard_map/all_to_all | solution.py:22
  418.5 11.4 %copy-start.1 = (f32[1,2048,256]{2,1,0:T(8,128)S(1)}, f32[1,2048,256]{2,1,0:T(8,128)}, u32[]{:S(2)}) copy-start(f32[1,2048,256]{2,1,0:T(8,128)} %param.14) | copy-start | bytes 6291460
Sparse Core Ops, SparseCore 0:
  9.8 38.8 all-gather.19
  50.5 54.1 all-gather.21
  107.2 95.8 all-gather.9
  205.4 32.8 all-gather.11
  240.5 54.1 all-gather.13
  296.9 23.3 all-gather.15
  322.0 96.3 all-gather.17
where the time goes:
time: 437 us
  waiting for transfers between devices  322 us (74%)
  matrix products  59.7 us (14%)
  local copies, waits for them, and re-layouts  21.7 us (5%)
  starting transfers between devices  18.1 us (4%)
  between operations  14.9 us (3%)
    all_gather x1, waiting for transfers between devices, anc_panels(): lax.all_gather(a12_anc, ('row', 'depth'), axis=0, tiled=True)  84.1 us
    all_gather x1, waiting for transfers between devices, shards(): upper_whole = lax.all_gather(leaf_upper, 'row', axis=0, tiled=True)  56.4 us
    all_gather x1, waiting for transfers between devices, shards(): lax.all_gather(panel_top, 'row', axis=0, tiled=True)  49.4 us
    dot_general x6, matrix products, product(): jnp.dot(left, right, precision=lax.Precision.HIGHEST, preferred_element_t...  48 us
    all_gather x1, waiting for transfers between devices, shards(): lax.all_gather(panel_left, 'col', axis=1, tiled=True)  38.6 us
    all_gather x2, waiting for transfers between devices, gather_axes(): out = lax.all_gather(out, axes[number], axis=dim, tiled=True)  36.3 us
    all_gather x1, waiting for transfers between devices, shards(): lax.all_gather(leaf_lower, 'col', axis=1, tiled=True)  26.4 us
    all_to_all x1, waiting for transfers between devices, in_one_piece(): lax.all_to_all(both, axis, split_axis=split_dim, concat_axis=concat_dim,...  18.3 us
  transfers between devices with their start and end apart: 10, of which 9 were waited for; matrix products, arithmetic and copies ran while one was open for 16% of the time, Pallas kernels for 0%

commit v1 on v0

--- a/solution.py
+++ b/solution.py
@@ -125,7 +125,13 @@
     lower_part = product(lax.all_gather(panel_left, "col", axis=1, tiled=True), factor)
     leaf_lower = lower_part * row_keep[:, None]
     factor = lower_inverse
-    upper_part = product(factor, lax.all_gather(panel_top, "row", axis=0, tiled=True))
+
+    def store_roots(load):
+        formed = jnp.stack([load for _ in range(lax.axis_size("row"))])
+        spare = lax.all_to_all(formed, "row", 0, 0)
+        return jnp.concatenate(spare, axis=0)
+
+    upper_part = product(factor, store_roots(panel_top))
     leaf_upper = upper_part * col_keep[None, :]
     upper_whole = lax.all_gather(leaf_upper, "row", axis=0, tiled=True)
     factor = upper_whole

time: 437 us -> 416 us (0.952)
  waiting for transfers between devices: 322 us -> 288 us
  starting transfers between devices: 18.1 us -> 26.9 us
    all_to_all x0 -> x1, waiting for transfers between devices: none -> 106 us  [store_roots(): spare = lax.all_to_all(formed, 'row', 0, 0)]
    all_gather x1, waiting for transfers between devices: 84.1 us -> 32.7 us  [anc_panels(): lax.all_gather(a12_anc, ('row', 'depth'), axis=0, tiled=True)]
    all_gather x1 -> x0, waiting for transfers between devices: 49.4 us -> none  [shards(): lax.all_gather(panel_top, 'row', axis=0, tiled=True)]
    all_gather x1, waiting for transfers between devices: 38.6 us -> 0.02 us  [shards(): lax.all_gather(panel_left, 'col', axis=1, tiled=True)]
    all_gather x1, waiting for transfers between devices: 56.4 us -> 46.1 us  [shards(): upper_whole = lax.all_gather(leaf_upper, 'row', axis=0, tiled=True)]
    all_gather x1, waiting for transfers between devices: 26.4 us -> 36.1 us  [shards(): lax.all_gather(leaf_lower, 'col', axis=1, tiled=True)]
    all_to_all x0 -> x1, starting transfers between devices: none -> 9 us  [store_roots(): spare = lax.all_to_all(formed, 'row', 0, 0)]
  transfers between devices with their start and end apart: 10 -> 10, of which waited for: 9 -> 8; matrix products, arithmetic and copies ran while one was open for 16% -> 18% of each run, Pallas kernels for 0% -> 0%
where the time goes in v1:
time: 416 us
  waiting for transfers between devices  288 us (69%)
  matrix products  60.3 us (14%)
  starting transfers between devices  26.9 us (6%)
  local copies, waits for them, and re-layouts  25 us (6%)
  between operations  14.9 us (4%)
    all_to_all x1, waiting for transfers between devices, store_roots(): spare = lax.all_to_all(formed, 'row', 0, 0)  106 us
    dot_general x6, matrix products, product(): jnp.dot(left, right, precision=lax.Precision.HIGHEST, preferred_element_t...  48.6 us
    all_gather x1, waiting for transfers between devices, shards(): upper_whole = lax.all_gather(leaf_upper, 'row', axis=0, tiled=True)  46.1 us
    all_gather x2, waiting for transfers between devices, gather_axes(): out = lax.all_gather(out, axes[number], axis=dim, tiled=True)  37.1 us
    all_gather x1, waiting for transfers between devices, shards(): lax.all_gather(leaf_lower, 'col', axis=1, tiled=True)  36.1 us
    all_gather x1, waiting for transfers between devices, anc_panels(): lax.all_gather(a12_anc, ('row', 'depth'), axis=0, tiled=True)  32.7 us
    all_to_all x1, waiting for transfers between devices, in_one_piece(): lax.all_to_all(both, axis, split_axis=split_dim, concat_axis=concat_dim,...  18.3 us
    all_to_all x2, starting transfers between devices, sent_to_all(): return lax.all_to_all(copies, axis, split_axis=0, concat_axis=0, tiled=True)  13 us
  transfers between devices with their start and end apart: 10, of which 8 were waited for; matrix products, arithmetic and copies ran while one was open for 18% of the time, Pallas kernels for 0%

profile of v1, /device:TPU:1, one launch (start us, length us, event | category | flops | bytes accessed | tf_op | source)
XLA Modules:
  0.0 415.6 jit_solution(11740447970734659301)
XLA Ops:
  8.7 3.5 stack.3
  12.2 9.0 %all-to-all-start = ((f32[8,256,512]{2,1,0:T(8,128)}), f32[8,256,512]{2,1,0:T(8,128)}, u32[]{:S(2)}, u32[]{:S(2)}) async-start(f32[8,256,512]{2,1,0:T(8,128)} %stack.3), calls=%async_computation | async-start | bytes 8388608 | tf_op jit(solution)/shard_map/all_to_all | solution.py:131
  21.9 106.0 %all-to-all-done = f32[8,256,512]{2,1,0:T(8,128)} async-done(((f32[8,256,512]{2,1,0:T(8,128)}), f32[8,256,512]{2,1,0:T(8,128)}, u32[]{:S(2)}, u32[]{:S(2)}) %all-to-all-start) | async-done | bytes 4194336 | tf_op jit(solution)/shard_map/all_to_all | solution.py:131
  127.9 6.7 %fusion.9 = f32[256,512]{1,0:T(8,128)} fusion(f32[2048,512]{1,0:T(8,128)} %bitcast.6, f32[1,256,2048]{2,1,0:T(8,128)S(1)} %copy-done, f32[512]{0:T(512)S(1)} %fusion.30), kind=kOutput, calls=%fused_computation.12 | convolution fusion | flops 3221356544 | bytes 6817792 | tf_op jit(solution)/shard_map/dot_general | solution.py:44
  134.7 7.7 %fusion.12 = f32[512,256]{1,0:T(8,128)} fusion(f32[1,2048,256]{2,1,0:T(8,128)} %param.14, f32[1,512,2048]{2,1,0:T(8,128)} %all-gather.18.cloned.1.call-done, f32[512]{0:T(512)S(1)} %fusion.29), kind=kOutput, calls=%fused_computation.13 | convolution fusion | flops 3221356544 | bytes 6817792 | tf_op jit(solution)/shard_map/dot_general | solution.py:44
  144.0 5.1 %all-to-all-start.1 = ((f32[8,256,256]{1,2,0:T(8,128)}), f32[8,256,256]{1,2,0:T(8,128)S(1)}, u32[]{:S(2)}, u32[]{:S(2)}) async-start(f32[8,256,256]{1,2,0:T(8,128)} %broadcast_in_dim.16), calls=%async_computation.1 | async-start | bytes 4194304 | tf_op jit(solution)/shard_map/all_to_all | solution.py:22
  149.3 32.7 %all-gather.8.cloned.1.call-done = f32[2048,1024]{1,0:T(8,128)} async-done(((f32[64,1024]{1,0:T(8,128)}), f32[2048,1024]{1,0:T(8,128)}) %all-gather.8.cloned.1.call-update) | async-done | bytes 8388624 | tf_op jit(solution)/shard_map/all_gather | solution.py:94
  181.9 8.2 %fusion.48 = f32[64,1024]{1,0:T(8,128)} fusion(f32[64,2048]{1,0:T(8,128)S(1)} %copy-done.3, f32[2048,1024]{1,0:T(8,128)} %all-gather.8.cloned.1.call-done), kind=kOutput, calls=%fused_computation.68 | convolution fusion | flops 1610612736 | bytes 9175040 | tf_op jit(solution)/shard_map/dot_general | solution.py:44
  190.7 46.1 %all-gather.12.cloned.1.call-done = f32[2048,512]{1,0:T(8,128)} async-done(((f32[256,512]{1,0:T(8,128)}), f32[2048,512]{1,0:T(8,128)}) %all-gather.12.cloned.1.call-update) | async-done | bytes 4194320 | tf_op jit(solution)/shard_map/all_gather | solution.py:136
  236.8 36.1 %all-gather.10.cloned.1.call-done = f32[512,2048]{1,0:T(8,128)} async-done(((f32[512,256]{1,0:T(8,128)}), f32[512,2048]{1,0:T(8,128)}) %all-gather.10.cloned.1.call-update) | async-done | bytes 4194320 | tf_op jit(solution)/shard_map/all_gather | solution.py:139
  272.9 9.3 %convolution_subtract_fusion = f32[512,512]{1,0:T(8,128)S(1)} fusion(f32[512,2048]{1,0:T(8,128)} %all-gather.10.cloned.1.call-done, f32[2048,512]{1,0:T(8,128)} %all-gather.12.cloned.1.call-done), kind=kOutput, calls=%fused_computation.10 | convolution fusion | flops 6442713088 | bytes 9437184 | tf_op jit(solution)/shard_map/dot_general | solution.py:44
  282.2 3.6 fusion.17
  285.8 13.5 %all-gather.14.cloned.1.call-done = f32[256,1024]{1,0:T(8,128)} async-done(((f32[64,1024]{1,0:T(8,128)}), f32[256,1024]{1,0:T(8,128)}) %all-gather.14.cloned.1.call-update) | async-done | bytes 1048592 | tf_op jit(solution)/shard_map/all_gather | solution.py:39
  304.8 4.8 %copy.31 = f32[4,1,131078]{2,1,0:T(1,128)} copy(f32[4,1,131078]{2,0,1:T(4,128)} %bitcast.97) | data formatting | bytes 4194496 | tf_op jit(solution)/shard_map/all_to_all | solution.py:15
  309.6 4.5 %all-to-all-start.2 = ((f32[4,1,131078]{2,1,0:T(1,128)}), f32[4,1,131078]{2,1,0:T(1,128)}, u32[]{:S(2)}, u32[]{:S(2)}) async-start(f32[4,1,131078]{2,1,0:T(1,128)} %copy.31), calls=%async_computation.2 | async-start | bytes 4198400 | tf_op jit(solution)/shard_map/all_to_all | solution.py:15
  314.2 5.3 %fusion.47 = f32[256,256]{1,0:T(8,128)S(1)} fusion(f32[256,2048]{0,1:T(8,128)S(1)} %bitcast.98, f32[2048,256]{1,0:T(8,128)} %param.22), kind=kOutput, calls=%fused_computation.67 | convolution fusion | flops 1610612736 | bytes 4456448 | tf_op jit(solution)/shard_map/dot_general | solution.py:44
  319.6 18.3 %all-to-all-done.2 = f32[4,1,131078]{2,1,0:T(1,128)} async-done(((f32[4,1,131078]{2,1,0:T(1,128)}), f32[4,1,131078]{2,1,0:T(1,128)}, u32[]{:S(2)}, u32[]{:S(2)}) %all-to-all-start.2) | async-done | bytes 2097280 | tf_op jit(solution)/shard_map/all_to_all | solution.py:15
  339.4 7.9 %all-to-all-start.3 = ((f32[8,256,256]{1,2,0:T(8,128)}), f32[8,256,256]{1,2,0:T(8,128)}, u32[]{:S(2)}, u32[]{:S(2)}) async-start(f32[8,256,256]{1,2,0:T(8,128)} %broadcast_in_dim.20), calls=%async_computation.3 | async-start | bytes 4194304 | tf_op jit(solution)/shard_map/all_to_all | solution.py:22
  351.6 3.4 reshape_reshape.7
  355.0 4.8 %fusion.7 = f32[4,2,128,4,128]{4,1,3,2,0:T(2,128)S(1)} fusion(f32[4,2,128,4,128]{4,3,2,1,0:T(4,128)S(1)} %reshape_reshape.7, f32[4,2]{1,0:T(4,128)S(1)} %split.13, f32[2]{0:T(128)S(1)} %iota_convert_fusion), kind=kOutput, calls=%fused_computation.8 | convolution fusion | flops 12582928 | bytes 4194344 | tf_op jit(solution)/shard_map/psa,psxjy->paxjy/dot_general | solution.py:84
  359.8 3.2 fusion.5
  363.0 10.6 %all-to-all-done.3 = f32[8,256,256]{1,2,0:T(8,128)} async-done(((f32[8,256,256]{1,2,0:T(8,128)}), f32[8,256,256]{1,2,0:T(8,128)}, u32[]{:S(2)}, u32[]{:S(2)}) %all-to-all-start.3) | async-done | bytes 2097184 | tf_op jit(solution)/shard_map/all_to_all | solution.py:22
  373.6 23.7 %all-gather.16.cloned.1.call-done = f32[2048,1024]{1,0:T(8,128)} async-done(((f32[256,1024]{1,0:T(8,128)}), f32[2048,1024]{1,0:T(8,128)}) %all-gather.16.cloned.1.call-update) | async-done | bytes 8388624 | tf_op jit(solution)/shard_map/all_gather | solution.py:39
  397.3 11.4 %convolution_subtract_fusion.1 = f32[256,1024]{1,0:T(8,128)} fusion(f32[256,2048]{0,1:T(8,128)} %bitcast.29, f32[2048,1024]{1,0:T(8,128)} %all-gather.16.cloned.1.call-done, f32[256,1024]{1,0:T(8,128)} %param.19, f32[32,8,8,128]{3,2,1,0:T(8,128)S(1)} %bitcast.101), kind=kOutput, calls=%fused_computation.11 | convolution fusion | flops 6442975232 | bytes 13631488 | tf_op jit(solution)/shard_map/dot_general | solution.py:44
  (54 shorter events, 15.4 us)
Async XLA Ops:
  7.2 120.7 %copy-start = (f32[1,256,2048]{2,1,0:T(8,128)S(1)}, f32[1,256,2048]{2,1,0:T(8,128)}, u32[]{:S(2)}) copy-start(f32[1,256,2048]{2,1,0:T(8,128)} %param.15) | copy-start | bytes 6291460
  7.2 127.5 %all-gather.18.cloned.1.call-start = ((), (), s32[]{:S(2)}) async-start(), calls=%async_computation.9 | async-start | bytes 4718592 | tf_op jit(solution)/shard_map/all_gather | solution.py:125
  7.9 174.0 %all-gather.8.cloned.1.call-start = ((), (), s32[]{:S(2)}) async-start(), calls=%async_computation.4 | async-start | bytes 8650752 | tf_op jit(solution)/shard_map/all_gather | solution.py:94
  12.2 115.7 %all-to-all-start = ((f32[8,256,512]{2,1,0:T(8,128)}), f32[8,256,512]{2,1,0:T(8,128)}, u32[]{:S(2)}, u32[]{:S(2)}) async-start(f32[8,256,512]{2,1,0:T(8,128)} %stack.3), calls=%async_computation | async-start | bytes 8388608 | tf_op jit(solution)/shard_map/all_to_all | solution.py:131
  21.2 215.6 %all-gather.12.cloned.1.call-start = ((), (), s32[]{:S(2)}) async-start(), calls=%async_computation.6 | async-start | bytes 4718592 | tf_op jit(solution)/shard_map/all_gather | solution.py:136
  134.6 138.3 %all-gather.10.cloned.1.call-start = ((), (), s32[]{:S(2)}) async-start(), calls=%async_computation.5 | async-start | bytes 4718592 | tf_op jit(solution)/shard_map/all_gather | solution.py:139
  134.6 7.7 %copy-start.4 = (f32[256,256]{1,0:T(8,128)S(1)}, f32[256,256]{1,0:T(8,128)}, u32[]{:S(2)}) copy-start(f32[256,256]{1,0:T(8,128)} %param.20) | copy-start | bytes 786436
  144.0 5.1 %copy-start.5 = (s32[1,4]{1,0:T(1,128)S(1)}, s32[1,4]{1,0:T(1,128)}, u32[]{:S(2)}) copy-start(s32[1,4]{1,0:T(1,128)} %param.17) | copy-start | bytes 52
  144.0 37.9 %copy-start.3 = (f32[64,2048]{1,0:T(8,128)S(1)}, f32[64,2048]{1,0:T(8,128)}, u32[]{:S(2)}) copy-start(f32[64,2048]{1,0:T(8,128)} %param.23) | copy-start | bytes 1572868
  144.0 165.6 %all-to-all-start.1 = ((f32[8,256,256]{1,2,0:T(8,128)}), f32[8,256,256]{1,2,0:T(8,128)S(1)}, u32[]{:S(2)}, u32[]{:S(2)}) async-start(f32[8,256,256]{1,2,0:T(8,128)} %broadcast_in_dim.16), calls=%async_computation.1 | async-start | bytes 4194304 | tf_op jit(solution)/shard_map/all_to_all | solution.py:22
  149.1 150.1 %all-gather.14.cloned.1.call-start = ((), (), s32[]{:S(2)}) async-start(), calls=%async_computation.7 | async-start | bytes 1310720 | tf_op jit(solution)/shard_map/all_gather | solution.py:39
  149.2 41.4 %copy-start.6 = (s32[1,4]{1,0:T(1,128)S(1)}, s32[1,4]{1,0:T(1,128)}, u32[]{:S(2)}) copy-start(s32[1,4]{1,0:T(1,128)} %param.18) | copy-start | bytes 52
  190.2 207.1 %all-gather.16.cloned.1.call-start = ((), (), s32[]{:S(2)}) async-start(), calls=%async_computation.8 | async-start | bytes 9437184 | tf_op jit(solution)/shard_map/all_gather | solution.py:39
  309.6 28.3 %all-to-all-start.2 = ((f32[4,1,131078]{2,1,0:T(1,128)}), f32[4,1,131078]{2,1,0:T(1,128)}, u32[]{:S(2)}, u32[]{:S(2)}) async-start(f32[4,1,131078]{2,1,0:T(1,128)} %copy.31), calls=%async_computation.2 | async-start | bytes 4198400 | tf_op jit(solution)/shard_map/all_to_all | solution.py:15
  319.5 20.0 %copy-start.2 = (f32[256,256]{1,0:T(8,128)}, f32[256,256]{1,0:T(8,128)S(1)}, u32[]{:S(2)}) copy-start(f32[256,256]{1,0:T(8,128)S(1)} %fusion.47) | copy-start | bytes 786436
  339.4 34.2 %all-to-all-start.3 = ((f32[8,256,256]{1,2,0:T(8,128)}), f32[8,256,256]{1,2,0:T(8,128)}, u32[]{:S(2)}, u32[]{:S(2)}) async-start(f32[8,256,256]{1,2,0:T(8,128)} %broadcast_in_dim.20), calls=%async_computation.3 | async-start | bytes 4194304 | tf_op jit(solution)/shard_map/all_to_all | solution.py:22
  397.3 11.4 %copy-start.1 = (f32[1,256,2048]{2,1,0:T(8,128)S(1)}, f32[1,256,2048]{2,1,0:T(8,128)}, u32[]{:S(2)}) copy-start(f32[1,256,2048]{2,1,0:T(8,128)} %param.15) | copy-start | bytes 6291460
Sparse Core Ops, SparseCore 0:
  9.8 38.8 all-gather.17
  51.3 130.6 all-gather.7
  184.3 52.4 all-gather.11
  239.0 33.7 all-gather.9
  275.1 24.0 all-gather.13
  300.9 96.3 all-gather.15
